TPU v7x, 32 devices: a 4x4x1 block of a 4x4x8 slice. The times are simulated.
32 devices in a mesh: dp: 1 (over z), sp: 4 (over y), tp: 8 (over x, core).
Axes of the slice: x: 4, y: 4, z: 1, core: 2. Of those that a mesh axis runs over, the one named last changes fastest.
The devices are a block of a 4x4x8 slice.
Arguments:
- x_in: bfloat16 [32768, 4096], P(('dp', 'sp', 'tp'))
- seg_ids: int32 [32768], P(('dp', 'sp', 'tp'))
- w_zx: bfloat16 [4096, 2, 8192], P(None, None, 'tp')
- w_bc: bfloat16 [4096, 2, 1024], P(None, None, 'tp')
- w_dt: bfloat16 [4096, 128], P(None, 'tp')
- conv_x: bfloat16 [4, 8192], P(None, 'tp')
- conv_bc: bfloat16 [4, 2, 1024], P(None, None, 'tp')
- bias_x: bfloat16 [8192], P('tp')
- bias_bc: bfloat16 [2, 1024], P(None, 'tp')
- a_log: float32 [128], P('tp')
- dt_bias: float32 [128], P('tp')
- d_skip: float32 [128], P('tp')
- norm_w: bfloat16 [8192], P('tp')
- w_out: bfloat16 [8192, 4096], P('tp')
Outputs:
- output: bfloat16 [32768, 4096], P(('dp', 'sp', 'tp'))
All inputs are finite; a program needn't handle non-finite values.
Results may differ from a plain program's by a relative error of at most 0.00658122.
Values are sent between devices in bfloat16 or wider.
A program may use at most 768 MiB of HBM per device.

v0:
```python
import math
import jax
import jax.numpy as jnp
from jax import lax
from jax.sharding import PartitionSpec as P

SSD_TILE = 256
CONV_WIDTH = 4
STATE_DIM = 128
NORM_EPS = 1e-5


def causal_conv(pre_rows, tail_rows, seg_rows, seg_tail, conv_w, conv_b):
    row_count = pre_rows.shape[0]
    padded = jnp.concatenate([tail_rows, pre_rows], axis=0)
    seg_pad = jnp.concatenate([seg_tail, seg_rows], axis=0)
    conv_acc = conv_b.astype(jnp.float32)
    for tap_idx in range(CONV_WIDTH):
        keep_tap = (seg_pad[tap_idx:tap_idx + row_count] == seg_rows)[:, None]
        tap_term = padded[tap_idx:tap_idx + row_count].astype(jnp.float32) * conv_w[tap_idx].astype(jnp.float32)
        conv_acc = conv_acc + jnp.where(keep_tap, tap_term, 0.0)
    return jax.nn.silu(conv_acc).astype(jnp.bfloat16)


def ssd_tile(state, tile_in, skip_gain):
    x_ssm, b_ssm, c_ssm, dt_val, log_a, seg_rows, seg_prev = tile_in
    row_count = x_ssm.shape[0]
    last_row = row_count - 1
    cum_log = jnp.cumsum(log_a, axis=0)
    causal = jnp.arange(row_count)[:, None] >= jnp.arange(row_count)[None, :]
    same_doc = ((seg_rows[:, None] == seg_rows[None, :]) & causal)[:, :, None, None]
    decay = jnp.where(same_doc, jnp.exp(jnp.where(same_doc, cum_log[:, None] - cum_log[None, :], 0.0)), 0.0)
    scores = jnp.einsum('tgn,sgn->tsg', c_ssm, b_ssm, preferred_element_type=jnp.float32)
    mix_mat = scores[..., None] * decay * dt_val[None]
    y_ssm = jnp.einsum('tsgr,sgrp->tgrp', mix_mat, x_ssm, preferred_element_type=jnp.float32)
    keep_in = (seg_rows == seg_prev)[:, None, None]
    in_fac = jnp.where(keep_in, jnp.exp(cum_log), 0.0)
    y_ssm = y_ssm + jnp.einsum('tgn,grpn->tgrp', c_ssm, state, preferred_element_type=jnp.float32) * in_fac[..., None]
    y_ssm = y_ssm + skip_gain[None, :, :, None] * x_ssm.astype(jnp.float32)
    keep_end = (seg_rows == seg_rows[last_row])[:, None, None]
    end_w = jnp.where(keep_end, jnp.exp(cum_log[last_row][None] - cum_log), 0.0) * dt_val
    carry_fac = jnp.where(seg_rows[last_row] == seg_prev, jnp.exp(cum_log[last_row]), 0.0)
    new_state = carry_fac[:, :, None, None] * state + jnp.einsum('sgrp,sgn->grpn', x_ssm * end_w[..., None], b_ssm, preferred_element_type=jnp.float32)
    return new_state, y_ssm


def block_ssd(x_ssm, b_ssm, c_ssm, dt_val, log_a, seg_rows, seg_prev, skip_gain):
    row_count, groups, per_group, head_dim = x_ssm.shape
    tile_size = math.gcd(row_count, SSD_TILE)
    n_tiles = row_count // tile_size
    seg_shift = jnp.concatenate([seg_prev[None], seg_rows[:-1]])
    tile_prev = seg_shift.reshape(n_tiles, tile_size)[:, 0]
    tiles_in = (x_ssm.reshape(n_tiles, tile_size, groups, per_group, head_dim), b_ssm.reshape(n_tiles, tile_size, groups, STATE_DIM), c_ssm.reshape(n_tiles, tile_size, groups, STATE_DIM), dt_val.reshape(n_tiles, tile_size, groups, per_group), log_a.reshape(n_tiles, tile_size, groups, per_group), seg_rows.reshape(n_tiles, tile_size), tile_prev)

    def body(state, step_in):
        return ssd_tile(state, step_in, skip_gain)

    init_state = jnp.zeros((groups, per_group, head_dim, STATE_DIM), jnp.float32)
    end_state, y_tiles = lax.scan(body, init_state, tiles_in)
    return end_state, y_tiles.reshape(row_count, groups, per_group, head_dim)


def gate_norm(y_ssm, z_gate, norm_w):
    row_count, groups, per_group, head_dim = y_ssm.shape
    group_size = per_group * head_dim
    gated = y_ssm.reshape(row_count, groups, group_size) * jax.nn.silu(z_gate.astype(jnp.float32)).reshape(row_count, groups, group_size)
    normed = gated * lax.rsqrt(jnp.mean(gated * gated, axis=-1, keepdims=True) + NORM_EPS)
    return (normed.reshape(row_count, groups * group_size) * norm_w.astype(jnp.float32)).astype(jnp.bfloat16)


def chain_state(end_state, block_decay, seq_axis, n_blocks):
    dev_index = lax.axis_index(seq_axis)
    to_next = [(src_dev, src_dev + 1) for src_dev in range(n_blocks - 1)]
    state_in = lax.ppermute(end_state, seq_axis, to_next)
    decay_in = jnp.where(dev_index == 0, 1.0, lax.ppermute(block_decay, seq_axis, to_next))
    for step_idx in range((n_blocks - 1).bit_length()):
        hop_span = 2 ** step_idx
        hop_perm = [(src_dev, src_dev + hop_span) for src_dev in range(n_blocks - hop_span)]
        prev_state = lax.ppermute(state_in, seq_axis, hop_perm)
        prev_decay = lax.ppermute(decay_in, seq_axis, hop_perm)
        has_prev = dev_index >= hop_span
        state_in = jnp.where(has_prev, decay_in[:, :, None, None] * prev_state + state_in, state_in)
        decay_in = jnp.where(has_prev, decay_in * prev_decay, decay_in)
    return state_in


def local_layer(x_blk, seg_blk, weights, seq_axis, n_blocks):
    w_zx, w_bc, w_dt, conv_x, conv_bc, bias_x, bias_bc, a_log, dt_bias, d_skip, norm_w, w_out = weights
    row_count = x_blk.shape[0]
    inner_dim = w_zx.shape[2]
    group_width = w_bc.shape[2]
    heads = w_dt.shape[1]
    groups = group_width // STATE_DIM
    per_group = heads // groups
    head_dim = inner_dim // heads
    halo_len = CONV_WIDTH - 1
    zx_proj = jnp.einsum('ld,dkc->lkc', x_blk, w_zx, preferred_element_type=jnp.float32).astype(jnp.bfloat16)
    bc_pre = jnp.einsum('ld,dkc->lkc', x_blk, w_bc, preferred_element_type=jnp.float32).astype(jnp.bfloat16).reshape(row_count, 2 * group_width)
    dt_raw = jnp.dot(x_blk, w_dt, preferred_element_type=jnp.float32).astype(jnp.bfloat16)
    x_pre = zx_proj[:, 1]
    to_next = [(src_dev, src_dev + 1) for src_dev in range(n_blocks - 1)]
    tail_x = lax.ppermute(x_pre[row_count - halo_len:], seq_axis, to_next)
    tail_bc = lax.ppermute(bc_pre[row_count - halo_len:], seq_axis, to_next)
    tail_seg = lax.ppermute(seg_blk[row_count - halo_len:], seq_axis, to_next)
    x_act = causal_conv(x_pre, tail_x, seg_blk, tail_seg, conv_x, bias_x)
    bc_act = causal_conv(bc_pre, tail_bc, seg_blk, tail_seg, conv_bc.reshape(CONV_WIDTH, 2 * group_width), bias_bc.reshape(2 * group_width))
    x_ssm = x_act.reshape(row_count, groups, per_group, head_dim)
    b_ssm = bc_act[:, :group_width].reshape(row_count, groups, STATE_DIM)
    c_ssm = bc_act[:, group_width:].reshape(row_count, groups, STATE_DIM)
    dt_val = jax.nn.softplus(dt_raw.astype(jnp.float32) + dt_bias).reshape(row_count, groups, per_group)
    log_a = -jnp.exp(a_log).reshape(groups, per_group) * dt_val
    seg_prev = tail_seg[halo_len - 1]
    end_state, y_local = block_ssd(x_ssm, b_ssm, c_ssm, dt_val, log_a, seg_blk, seg_prev, d_skip.reshape(groups, per_group))
    cum_blk = jnp.cumsum(log_a, axis=0)
    block_decay = jnp.where(seg_blk[row_count - 1] == seg_prev, jnp.exp(cum_blk[row_count - 1]), 0.0)
    state_in = chain_state(end_state, block_decay, seq_axis, n_blocks)
    keep_blk = (seg_blk == seg_prev)[:, None, None]
    corr_fac = jnp.where(keep_blk, jnp.exp(cum_blk), 0.0)
    y_ssm = y_local + jnp.einsum('tgn,grpn->tgrp', c_ssm, state_in, preferred_element_type=jnp.float32) * corr_fac[..., None]
    y_norm = gate_norm(y_ssm, zx_proj[:, 0], norm_w)
    return jnp.dot(y_norm, w_out, preferred_element_type=jnp.float32)


def solution(mesh):
    seq_blocks = mesh.shape['sp']
    token_spec = P(('dp', 'sp', 'tp'), None)
    seg_spec = P(('dp', 'sp', 'tp'))
    weight_specs = (P(None, None, 'tp'), P(None, None, 'tp'), P(None, 'tp'), P(None, 'tp'), P(None, None, 'tp'), P('tp'), P(None, 'tp'), P('tp'), P('tp'), P('tp'), P('tp'), P('tp', None))

    def body(x_loc, seg_loc, w_zx, w_bc, w_dt, conv_x, conv_bc, bias_x, bias_bc, a_log, dt_bias, d_skip, norm_w, w_out):
        x_blk = lax.all_gather(x_loc, 'tp', axis=0, tiled=True)
        seg_blk = lax.all_gather(seg_loc, 'tp', axis=0, tiled=True)
        weights = (w_zx, w_bc, w_dt, conv_x, conv_bc, bias_x, bias_bc, a_log, dt_bias, d_skip, norm_w, w_out)
        out_part = local_layer(x_blk, seg_blk, weights, 'sp', seq_blocks)
        out_loc = lax.psum_scatter(out_part, 'tp', scatter_dimension=0, tiled=True)
        return (x_loc.astype(jnp.float32) + out_loc).astype(jnp.bfloat16)

    return jax.shard_map(body, mesh=mesh, in_specs=(token_spec, seg_spec) + weight_specs, out_specs=token_spec, check_vma=False)
```

profile of v0, /device:TPU:97, one launch (start us, length us, event | category | flops | bytes accessed | tf_op | source)
XLA Modules:
  0.0 2916.3 jit_solution(18064021058108982179)
XLA Ops:
  7.4 19.0 all_gather.6
  26.4 3.8 collective-permute-start
  40.3 267.8 %all-gather.2.cloned.1.call-done = bf16[8192,4096]{1,0:T(8,128)(2,1)} async-done(((bf16[1024,4096]{1,0:T(8,128)(2,1)}), bf16[8192,4096]{1,0:T(8,128)(2,1)}) %all-gather.2.cloned.1.call-update) | async-done | bytes 67108880 | tf_op jit(solution)/shard_map/all_gather | solution.py:131
  308.1 28.4 fusion.68
  337.7 3.9 collective-permute-start.2
  341.6 152.5 %fusion.58 = bf16[8192,2,1024]{2,0,1:T(8,128)(2,1)} fusion(bf16[8192,4096]{1,0:T(8,128)(2,1)} %all-gather.2.cloned.1.call-done, bf16[4096,2,1024]{2,1,0:T(2,128)(2,1)} %param.18), kind=kOutput, calls=%fused_computation.85 | convolution fusion | flops 137455730688 | bytes 117440512 | tf_op jit(solution)/shard_map/ld,dkc->lkc/dot_general | solution.py:97
  494.1 13.9 slice_bitcast_fusion.1
  508.0 25.7 broadcast_multiply_fusion
  534.6 6.4 copy.82
  542.9 6.4 copy.83
  549.3 2.6 collective-permute-start.1
  552.0 14.1 multiply_convert_fusion.1
  570.4 43.9 %multiply_convert_fusion = bf16[8192,1024]{1,0:T(8,128)(2,1)} fusion(bf16[8192,1024]{1,0:T(8,128)(2,1)} %slice_bitcast_fusion.1, bf16[3,1024]{1,0:T(4,128)(2,1)S(1)} %collective-permute-done.1, f32[1024]{0:T(1024)S(1)} %bitcast.270, f32[1024]{0:T(1024)S(1)} %bitcast.271, f32[1024]{0:T(1024)S(1)} %bitcast.269, f32[1024]{0:T(1024)S(1)} %bitcast.268, ...), kind=kLoop, calls=%fused_computation.82 | loop fusion | flops 243269632 | bytes 33605632 | tf_op jit(solution)/shard_map/convert_element_type | solution.py:22
  614.3 43.1 %reshape.407 = bf16[32,256,1,16,64]{4,3,1,0,2:T(8,128)(2,1)} reshape(bf16[8192,1024]{1,0:T(8,128)(2,1)} %multiply_convert_fusion) | data formatting | bytes 33554432 | tf_op jit(solution)/shard_map/reshape;reshape | solution.py:53
  657.4 37.5 %copy.86 = bf16[32,256,1,16,64]{1,4,3,2,0:T(8,128)(2,1)} copy(bf16[32,256,1,16,64]{4,3,1,0,2:T(8,128)(2,1)} %reshape.407) | data formatting | bytes 33554432
  694.9 1294.9 %while.13 = (s32[]{:T(128)}, f32[1,16,64,128]{3,2,1,0:T(8,128)S(1)}, f32[32,256,1,16,64]{1,0,4,3,2:T(8,128)}, s32[32,256]{1,0:T(8,128)}, s32[32]{0:T(128)S(1)}, ...) while((s32[]{:T(128)}, ...), condition=%wide.region_3.4_spmd.clone, body=%wide.region_0.3_spmd.clone.sunk | while | flops 293552704 | bytes 12430192 | solution.py:59
  711.0 24.4 dynamic_update_slice.6
  751.5 24.4 dynamic_update_slice.6
  792.0 24.4 dynamic_update_slice.6
  832.5 24.4 dynamic_update_slice.6
  873.0 24.4 dynamic_update_slice.6
  913.5 24.4 dynamic_update_slice.6
  954.0 24.4 dynamic_update_slice.6
  994.5 24.4 dynamic_update_slice.6
  1034.9 24.3 dynamic_update_slice.6
  1075.4 24.3 dynamic_update_slice.6
  1115.8 24.3 dynamic_update_slice.6
  1156.3 24.3 dynamic_update_slice.6
  1196.7 24.3 dynamic_update_slice.6
  1237.1 24.3 dynamic_update_slice.6
  1277.6 24.3 dynamic_update_slice.6
  1318.0 24.3 dynamic_update_slice.6
  1358.5 24.4 dynamic_update_slice.6
  1398.9 24.4 dynamic_update_slice.6
  1439.4 24.4 dynamic_update_slice.6
  1479.9 24.4 dynamic_update_slice.6
  1520.3 24.4 dynamic_update_slice.6
  1560.8 24.4 dynamic_update_slice.6
  1601.3 24.4 dynamic_update_slice.6
  1641.7 24.4 dynamic_update_slice.6
  1682.2 24.4 dynamic_update_slice.6
  1716.1 2.6 fusion.123
  1722.7 24.4 dynamic_update_slice.6
  1763.1 24.4 dynamic_update_slice.6
  1803.6 24.4 dynamic_update_slice.6
  1844.0 24.4 dynamic_update_slice.6
  1884.5 24.4 dynamic_update_slice.6
  1925.0 24.4 dynamic_update_slice.6
  1965.4 24.4 dynamic_update_slice.6
  1989.8 3.4 collective-permute-start.5
  1995.8 4.8 reduce-window.16
  2000.6 2.7 copy.98
  2004.0 3.4 collective-permute-start.6
  2007.7 31.3 %broadcast_select_fusion.3 = (f32[8192,1,16]{2,1,0:T(1,128)}, f32[8192,1,16]{2,1,0:T(1,128)S(1)}) fusion(pred[8192]{0:T(1024)(128)(4,1)S(1)} %copy-done.9, f32[16,1,8192]{0,1,2:T(1,128)} %bitcast.250, f32[16,1,8192]{0,1,2:T(1,128)S(1)} %bitcast.251), kind=kLoop, calls=%fused_computation.100 | loop fusion | flops 262144 | bytes 2105344 | tf_op jit(solution)/shard_map/jit(_where)/select_n | solution.py:118
  2042.0 4.3 collective-permute-start.7
  2047.7 2.8 copy.94
  2050.5 4.5 collective-permute-done.4
  2055.0 35.9 %reshape.374 = f32[8192,1,16,64]{0,3,2,1:T(8,128)} reshape(f32[32,256,1,16,64]{1,0,4,3,2:T(8,128)} %get-tuple-element.63) | data formatting | bytes 67108864 | tf_op jit(solution)/shard_map/reshape | solution.py:60
  2090.9 21.8 fusion.56
  2112.7 33.4 %copy.95 = f32[8192,1,1024]{2,0,1:T(8,128)} copy(f32[8192,1,1024]{0,2,1:T(8,128)} %bitcast.247) | data formatting | bytes 67108864 | tf_op jit(solution)/shard_map/reshape | solution.py:66
  2146.2 19.1 multiply_reduce_fusion
  2165.3 89.3 %fusion.63 = f32[8192,4096]{1,0:T(8,128)} fusion(bf16[1024,4096]{1,0:T(8,128)(2,1)} %param.29, f32[1024]{0:T(1024)S(1)} %convert_element_type.167, f32[8192]{0:T(1024)S(1)} %add_rsqrt_fusion, f32[8192,1,1024]{2,0,1:T(8,128)} %copy.95, bf16[8192,2,1024]{2,0,1:T(8,128)(2,1)} %fusion.58), kind=kOutput, calls=%fused_computation.88 | convolution fusion | flops 68794974208 | bytes 192974848 | tf_op jit(solution)/shard_map/dot_general | solution.py:121
  2254.7 642.6 %reduce-scatter.2.cloned.1.call-done = f32[1024,4096]{1,0:T(8,128)} async-done(((f32[8192,4096]{1,0:T(8,128)}), f32[1024,4096]{1,0:T(8,128)}) %reduce-scatter.2.cloned.1.call-update) | async-done | bytes 16777232 | tf_op jit(solution)/shard_map/reduce_scatter | solution.py:135
  2897.3 12.0 add_convert_fusion
  (959 shorter events, 496.3 us)
Async XLA Ops:
  6.5 301.5 %copy-start = (bf16[4096,2,128]{2,1,0:T(2,128)(2,1)S(1)}, bf16[4096,2,128]{2,1,0:T(2,128)(2,1)}, u32[]{:S(2)}) copy-start(bf16[4096,2,128]{2,1,0:T(2,128)(2,1)} %param.19) | copy-start | bytes 6291460
  6.6 301.5 %all-gather.2.cloned.1.call-start = ((), (), s32[]{:S(2)}) async-start(), calls=%async_computation.1 | async-start | bytes 75497472 | tf_op jit(solution)/shard_map/all_gather | solution.py:131
  7.3 2889.9 %reduce-scatter.2.cloned.1.call-start = ((), (), s32[]{:S(2)}) async-start(), calls=%async_computation.2 | async-start | bytes 150994944 | tf_op jit(solution)/shard_map/reduce_scatter | solution.py:135
  26.4 310.1 %copy-start.4 = (s32[8192]{0:T(1024)}, s32[8192]{0:T(1024)S(1)}, u32[]{:S(2)}) copy-start(s32[8192]{0:T(1024)S(1)} %all_gather.6) | copy-start | bytes 98308
  26.4 10.8 collective-permute-start
  337.7 214.1 %collective-permute-start.2 = (bf16[3,256]{1,0:T(4,128)(2,1)}, bf16[3,256]{1,0:T(4,128)(2,1)}, u32[]{:S(2)}, u32[]{:S(2)}) collective-permute-start(bf16[3,256]{1,0:T(4,128)(2,1)} %slice_bitcast_fusion.4), channel_id=1, source_target_pairs={{0,8},{8,16},{16,24},{1,9},{9,17},{17,25},{2,10},{10,18},{18,26},{... | collective-permute-start | bytes 4616 | tf_op jit(solution)/shard_map/ppermute | solution.py:103
  494.1 13.9 copy-start.5
  494.1 13.9 copy-start.10
  494.1 13.9 copy-start.11
  533.7 18.2 copy-start.6
  533.7 18.2 copy-start.7
  533.8 18.2 copy-start.8
  533.8 18.2 copy-start.18
  533.8 18.2 copy-start.19
  533.8 18.2 copy-start.20
  533.8 18.2 copy-start.21
  533.8 18.2 copy-start.23
  534.5 35.8 %copy-start.12 = (f32[1024]{0:T(1024)S(1)}, f32[1024]{0:T(1024)}, u32[]{:S(2)}) copy-start(f32[1024]{0:T(1024)} %convert_element_type.143) | copy-start | bytes 12292
  534.5 35.8 %copy-start.13 = (f32[1,1024]{1,0:T(1,128)S(1)}, f32[1,1024]{1,0:T(1,128)}, u32[]{:S(2)}) copy-start(f32[1,1024]{1,0:T(1,128)} %get-tuple-element.183) | copy-start | bytes 12292
  534.6 35.8 %copy-start.14 = (f32[1,1024]{1,0:T(1,128)S(1)}, f32[1,1024]{1,0:T(1,128)}, u32[]{:S(2)}) copy-start(f32[1,1024]{1,0:T(1,128)} %get-tuple-element.184) | copy-start | bytes 12292
  534.6 35.8 %copy-start.15 = (f32[1,1024]{1,0:T(1,128)S(1)}, f32[1,1024]{1,0:T(1,128)}, u32[]{:S(2)}) copy-start(f32[1,1024]{1,0:T(1,128)} %get-tuple-element.185) | copy-start | bytes 12292
  534.6 35.8 %copy-start.16 = (f32[1,1024]{1,0:T(1,128)S(1)}, f32[1,1024]{1,0:T(1,128)}, u32[]{:S(2)}) copy-start(f32[1,1024]{1,0:T(1,128)} %get-tuple-element.186) | copy-start | bytes 12292
  549.3 21.1 collective-permute-start.1
  566.1 1.9 copy-start.3
  657.4 37.5 %copy-start.2 = (f32[1,16,64,128]{3,2,1,0:T(8,128)S(1)}, f32[1,16,64,128]{3,2,1,0:T(8,128)}, u32[]{:S(2)}) copy-start(f32[1,16,64,128]{3,2,1,0:T(8,128)} %custom-call) | copy-start | bytes 1572868
  657.4 37.5 %copy-start.17 = (f32[16]{0:T(128)S(1)}, f32[16]{0:T(128)}, u32[]{:S(2)}) copy-start(f32[16]{0:T(128)} %param.27) | copy-start | bytes 196
  657.4 37.5 %copy-start.24 = (s32[32]{0:T(128)S(1)}, s32[32]{0:T(128)}, u32[]{:S(2)}) copy-start(s32[32]{0:T(128)} %slice_reduce_fusion.3) | copy-start | bytes 388
  694.9 1312.8 %copy-start.9 = (pred[8192]{0:T(1024)(128)(4,1)S(1)}, pred[8192]{0:T(1024)(128)(4,1)}, u32[]{:S(2)}) copy-start(pred[8192]{0:T(1024)(128)(4,1)} %get-tuple-element.182) | copy-start | bytes 24580
  1989.8 56.5 %copy-start.22 = (bf16[1024]{0:T(1024)(128)(2,1)S(1)}, bf16[1024]{0:T(1024)(128)(2,1)}, u32[]{:S(2)}) copy-start(bf16[1024]{0:T(1024)(128)(2,1)} %param.28) | copy-start | bytes 6148
  1989.8 14.2 collective-permute-start.5
  2004.0 37.9 %collective-permute-start.6 = (f32[1,16,64,128]{3,2,1,0:T(8,128)S(1)}, f32[1,16,64,128]{3,2,1,0:T(8,128)S(1)}, u32[]{:S(2)}, u32[]{:S(2)}) collective-permute-start(f32[1,16,64,128]{3,2,1,0:T(8,128)S(1)} %collective-permute-done.5), channel_id=1, source_target_pairs={{0,8},{8,16},{16,24},{1,9},{9,17},{17,25},{2,10},{10,18},{18,26},{... | collective-permute-start | bytes 1572872 | tf_op jit(solution)/shard_map/ppermute | solution.py:79
  2039.0 2.9 collective-permute-start.3
  2042.0 48.9 %collective-permute-start.7 = (f32[1,16,64,128]{3,2,1,0:T(8,128)S(1)}, f32[1,16,64,128]{3,2,1,0:T(8,128)S(1)}, u32[]{:S(2)}, u32[]{:S(2)}) collective-permute-start(f32[1,16,64,128]{3,2,1,0:T(8,128)S(1)} %add_select_fusion.1), channel_id=1, source_target_pairs={{0,16},{8,24},{1,17},{9,25},{2,18},{10,26},{3,19},{11,27},{4,20},{... | collective-permute-start | bytes 1572872 | tf_op jit(solution)/shard_map/ppermute | solution.py:79
  2046.4 8.7 collective-permute-start.4
  2254.7 654.6 %copy-start.1 = (bf16[4096,2,128]{2,1,0:T(2,128)(2,1)S(1)}, bf16[4096,2,128]{2,1,0:T(2,128)(2,1)}, u32[]{:S(2)}) copy-start(bf16[4096,2,128]{2,1,0:T(2,128)(2,1)} %param.19) | copy-start | bytes 6291460
Sparse Core Ops, SparseCore 0:
  9.0 299.0 all-gather.1
  2254.8 642.4 reduce-scatter.1
where the time goes:
time: 2950 us; the launch traced here: 2920 us
  local copies, waits for them, and re-layouts  1150 us (39%)
  waiting for transfers between devices  916 us (31%)
  matrix products  523 us (18%)
  other arithmetic  229 us (8%)
  loops' own time  42.3 us (1%)
    dynamic_update_slice x64, local copies, waits for them, and re-layouts, block_ssd(): end_state, y_tiles = lax.scan(body, init_state, tiles_in)  816 us
    reduce_scatter x1, waiting for transfers between devices, body(): out_loc = lax.psum_scatter(out_part, 'tp', scatter_dimension=0, tiled=True)  643 us
    all_gather x1, waiting for transfers between devices, body(): x_blk = lax.all_gather(x_loc, 'tp', axis=0, tiled=True)  268 us
    dot_general x1, matrix products, local_layer(): jnp.einsum('ld,dkc->lkc', x_blk, w_zx, preferred_element_type=jnp.float32)  152 us
    dot_general x1, matrix products, local_layer(): return jnp.dot(y_norm, w_out, preferred_element_type=jnp.float32)  89.3 us
    dot_general x32, matrix products, ssd_tile(): jnp.einsum('tsgr,sgrp->tgrp', mix_mat, x_ssm, preferred_element_type=jnp....  83 us
    dynamic_slice x128, local copies, waits for them, and re-layouts, block_ssd(): end_state, y_tiles = lax.scan(body, init_state, tiles_in)  70.9 us
  transfers between devices with their start and end apart: 10, of which 4 were waited for; matrix products, arithmetic and copies ran while one was open for 11% of the time, Pallas kernels for 0%

commit v1 on v0

v1 whole, which is shorter than its diff:
```python
import math, functools
import jax, jax.numpy as jnp
from jax import lax
from jax.sharding import PartitionSpec as P
from jax.experimental import pallas as pl
from jax.experimental.pallas import tpu as pltpu

F32, BF16 = jnp.float32, jnp.bfloat16
NEG = -1e30
LOG2E = 1.4426950408889634
CH = 128
NORM_EPS = 1e-5
CONV_WIDTH = 4
STATE_DIM = 128


def dotf(a, b):
    return jnp.dot(a, b, preferred_element_type=F32)


def split3_lanes(v, lane, heads):
    hi = v.astype(BF16).astype(F32)
    rest = v - hi
    mid = rest.astype(BF16).astype(F32)
    low = rest - mid
    part = jnp.where(lane < heads, hi, jnp.where(lane < 2 * heads, mid, jnp.where(lane < 3 * heads, low, 0.0)))
    return part.astype(BF16)


def ssd_kernel(xs_ref, bc_ref, dt_ref, comb_ref, row_ref, halo_ref, cw_ref, dtp_ref, dskip_ref, exp_ref,
               y_ref, c_ref, corr_ref, end_ref, dec_ref,
               state, prev, runcum, segp, *, heads, inner, ns):
    step = pl.program_id(0)
    rows = xs_ref.shape[0]
    n_sub = rows // CH
    hd = inner // heads
    width = inner + 2 * ns

    @pl.when(step == 0)
    def _():
        state[...] = jnp.zeros_like(state)
        runcum[...] = jnp.zeros_like(runcum)
        segp[...] = jnp.zeros_like(segp)
        prev[...] = jnp.zeros_like(prev)
        prev[CH - 8:, :] = halo_ref[...]

    it = lax.broadcasted_iota(jnp.int32, (CH, CH), 0)
    isx = lax.broadcasted_iota(jnp.int32, (CH, CH), 1)
    causal = it >= isx
    tri = jnp.where(causal, 1.0, 0.0).astype(BF16)
    tri3 = jnp.concatenate([tri, tri, tri], axis=1)
    half = lax.broadcasted_iota(jnp.int32, (CH, 2 * hd), 1) < hd
    for sub in range(n_sub):
        sl = pl.ds(sub * CH, CH)
        comb = comb_ref[sl, :]
        segb = comb >> 2
        dist = comb & 3
        shifts = []
        for j in (1, 2, 3):
            diag = isx - it
            keep = dist >= j
            in_cur = jnp.where((diag == -j) & keep, 1.0, 0.0)
            in_prev = jnp.where((diag == CH - j) & keep, 1.0, 0.0)
            shifts.append(jnp.concatenate([in_prev, in_cur], axis=1).astype(BF16))
        sh = jnp.concatenate(shifts, axis=0)

        def conv(cur, lo, hi):
            past = dotf(sh, jnp.concatenate([prev[:, lo:hi], cur], axis=0))
            acc = cur.astype(F32) * cw_ref[3:4, lo:hi] + cw_ref[4:5, lo:hi]
            for j in (1, 2, 3):
                acc = acc + past[(j - 1) * CH:j * CH] * cw_ref[3 - j:4 - j, lo:hi]
            prev[:, lo:hi] = cur
            return (acc + acc * jnp.tanh(acc)).astype(BF16)

        bc_act = conv(bc_ref[sl, :], inner, width)
        b_act = bc_act[:, :ns]
        c_act = bc_act[:, ns:]
        c_ref[sl, :] = c_act
        dt = dt_ref[sl, :].astype(F32) + dtp_ref[0:1, :]
        dt = jnp.maximum(dt, 0.0) + jnp.log1p(jnp.exp(-jnp.abs(dt)))
        la = dt * dtp_ref[1:2, :]
        hi3 = la.astype(BF16)
        r1 = la - hi3.astype(F32)
        mi3 = r1.astype(BF16)
        lo3 = (r1 - mi3.astype(F32)).astype(BF16)
        cum = dotf(tri3, jnp.concatenate([hi3, mi3, lo3], axis=0))
        l2dt = jnp.log2(dt)
        last = cum[CH - 1:CH, :]
        rt = (l2dt - cum).T
        seg_prev = segp[0:1, :]
        seg_last = segb[CH - 1:CH, :]
        mask = causal & (segb == row_ref[sub, :, :])
        scores = lax.dot_general(c_act, b_act, (((1,), (1,)), ((), ())), preferred_element_type=F32)
        wv = jnp.where(segb == seg_last, jnp.exp2(last - cum + l2dt), 0.0)
        fin = jnp.where(segb == seg_prev, jnp.exp2(cum), 0.0)
        carry = jnp.where(seg_last == seg_prev, jnp.exp2(last), 0.0)
        stack = jnp.concatenate([wv, fin, jnp.broadcast_to(carry, (8, CH))], axis=0)
        lane = lax.broadcasted_iota(jnp.int32, stack.shape, 1)
        stack = split3_lanes(stack, lane, heads)
        blk = 4 * hd
        for q in range(inner // blk):
            lo, hi = q * blk, (q + 1) * blk
            x_act = conv(xs_ref[sl, lo:hi], lo, hi)
            x_f = x_act.astype(F32)
            expd = dotf(stack, exp_ref[:, lo:hi])
            y_int = dotf(c_act, state[:, lo:hi].astype(BF16))
            y_base = y_int * expd[CH:2 * CH] + x_f * dskip_ref[0:1, lo:hi]
            xw = (x_f * expd[:CH]).astype(BF16)
            dstate = lax.dot_general(b_act, xw, (((0,), (0,)), ((), ())), preferred_element_type=F32)
            state[:, lo:hi] = state[:, lo:hi] * expd[2 * CH:2 * CH + 1] + dstate
            for p in range(2):
                mixes = []
                for h in (4 * q + 2 * p, 4 * q + 2 * p + 1):
                    arg = jnp.where(mask, cum[:, h:h + 1] + rt[h:h + 1, :], NEG)
                    mixes.append((scores * jnp.exp2(arg)).astype(BF16))
                lhs = jnp.concatenate(mixes, axis=1)
                xp = x_act[:, p * 2 * hd:(p + 1) * 2 * hd]
                zero = jnp.zeros_like(xp)
                rhs = jnp.concatenate([jnp.where(half, xp, zero), jnp.where(half, zero, xp)], axis=0)
                y_ref[sl, lo + p * 2 * hd:lo + (p + 1) * 2 * hd] = y_base[:, p * 2 * hd:(p + 1) * 2 * hd] + dotf(lhs, rhs)
        corr_ref[sl, :] = jnp.where(segb == 0, runcum[0:1, :] + cum, NEG)
        runcum[...] = runcum[...] + last
        segp[...] = jnp.broadcast_to(seg_last, segp.shape)

    @pl.when(step == pl.num_programs(0) - 1)
    def _():
        end_ref[...] = state[...]
        dec_ref[...] = jnp.where(segp[...] == 0, jnp.exp2(runcum[...]), 0.0)


def ssd_call(proj, comb, comb_row, halo, cw, dtp, dskip, expm, *, heads, inner, ns, rows=256):
    n_tok = proj.shape[0]
    width = inner + 2 * ns
    n_sub = rows // CH
    kern = functools.partial(ssd_kernel, heads=heads, inner=inner, ns=ns)
    full = lambda a: pl.BlockSpec(a.shape, lambda i: (0,) * a.ndim)
    return pl.pallas_call(
        kern,
        grid=(n_tok // rows,),
        in_specs=[
            pl.BlockSpec((rows, inner), lambda i: (i, 0)),
            pl.BlockSpec((rows, 2 * ns), lambda i: (i, inner // (2 * ns))),
            pl.BlockSpec((rows, CH), lambda i: (i, width // CH)),
            pl.BlockSpec((rows, CH), lambda i: (i, 0)),
            pl.BlockSpec((n_sub, 1, CH), lambda i: (i, 0, 0)),
            full(halo), full(cw), full(dtp), full(dskip), full(expm),
        ],
        out_specs=[
            pl.BlockSpec((rows, inner), lambda i: (i, 0)),
            pl.BlockSpec((rows, ns), lambda i: (i, 0)),
            pl.BlockSpec((rows, CH), lambda i: (i, 0)),
            pl.BlockSpec((ns, inner), lambda i: (0, 0)),
            pl.BlockSpec((8, CH), lambda i: (0, 0)),
        ],
        out_shape=[
            jax.ShapeDtypeStruct((n_tok, inner), F32),
            jax.ShapeDtypeStruct((n_tok, ns), BF16),
            jax.ShapeDtypeStruct((n_tok, CH), F32),
            jax.ShapeDtypeStruct((ns, inner), F32),
            jax.ShapeDtypeStruct((8, CH), F32),
        ],
        scratch_shapes=[
            pltpu.VMEM((ns, inner), F32),
            pltpu.VMEM((CH, width), BF16),
            pltpu.VMEM((8, CH), F32),
            pltpu.VMEM((8, CH), jnp.int32),
        ],
        compiler_params=pltpu.CompilerParams(dimension_semantics=("arbitrary",), vmem_limit_bytes=40 * 2**20),
        cost_estimate=pl.CostEstimate(flops=n_tok * 2 * 10**6, bytes_accessed=n_tok * 8000, transcendentals=0),
        name="ssd",
    )(proj, proj, proj, comb, comb_row, halo, cw, dtp, dskip, expm)


def gate_kernel(y_ref, c_ref, corr_ref, z_ref, st_ref, nw_ref, exp_ref, v_ref, *, heads, eps):
    rows = y_ref.shape[0]
    for sub in range(rows // CH):
        sl = pl.ds(sub * CH, CH)
        fac = jnp.exp2(corr_ref[sl, :])
        lane = lax.broadcasted_iota(jnp.int32, fac.shape, 1)
        fexp = dotf(split3_lanes(fac, lane, heads), exp_ref[...])
        y = y_ref[sl, :] + dotf(c_ref[sl, :], st_ref[...]) * fexp
        hz = z_ref[sl, :].astype(F32) * 0.5
        v = y * (hz + hz * jnp.tanh(hz))
        ms = jnp.mean(v * v, axis=-1, keepdims=True)
        v_ref[sl, :] = (v * lax.rsqrt(ms + eps) * nw_ref[0:1, :]).astype(BF16)


def gate_call(y, c, corr, z, st, nw, expm, *, heads, eps, rows=256):
    n_tok, inner = y.shape
    full = lambda a: pl.BlockSpec(a.shape, lambda i: (0,) * a.ndim)
    return pl.pallas_call(
        functools.partial(gate_kernel, heads=heads, eps=eps),
        grid=(n_tok // rows,),
        in_specs=[
            pl.BlockSpec((rows, inner), lambda i: (i, 0)),
            pl.BlockSpec((rows, c.shape[1]), lambda i: (i, 0)),
            pl.BlockSpec((rows, CH), lambda i: (i, 0)),
            pl.BlockSpec((rows, inner), lambda i: (i, 0)),
            full(st), full(nw), full(expm),
        ],
        out_specs=pl.BlockSpec((rows, inner), lambda i: (i, 0)),
        out_shape=jax.ShapeDtypeStruct((n_tok, inner), BF16),
        compiler_params=pltpu.CompilerParams(dimension_semantics=("arbitrary",), vmem_limit_bytes=40 * 2**20),
        cost_estimate=pl.CostEstimate(flops=n_tok * 10**6 // 2, bytes_accessed=n_tok * 8000, transcendentals=0),
        name="gate",
    )(y, c, corr, z, st, nw, expm)


def head_tables(heads, inner, a_log, dt_bias, d_skip):
    hd = inner // heads
    reps = CH // heads
    zeros = jnp.zeros((6, CH), F32)
    dtp = jnp.concatenate([jnp.tile(dt_bias, reps)[None], jnp.tile(-jnp.exp(a_log) * LOG2E, reps)[None], zeros], axis=0)
    dskip = jnp.repeat(d_skip, hd)[None]
    lane = jnp.arange(CH)[:, None]
    col_head = jnp.arange(inner)[None, :] // hd
    expm = ((lane < 3 * heads) & (lane % heads == col_head)).astype(BF16)
    return dtp, dskip, expm


def solution(mesh):
    seq_blocks = mesh.shape['sp']
    head_shards = mesh.shape['tp']
    token_spec = P(('dp', 'sp', 'tp'), None)
    seg_spec = P(('dp', 'sp', 'tp'))
    weight_specs = (P(None, None, 'tp'), P(None, None, 'tp'), P(None, 'tp'), P(None, 'tp'), P(None, None, 'tp'), P('tp'), P(None, 'tp'), P('tp'), P('tp'), P('tp'), P('tp'), P('tp', None))

    def body(x_loc, seg_loc, w_zx, w_bc, w_dt, conv_x, conv_bc, bias_x, bias_bc, a_log, dt_bias, d_skip, norm_w, w_out):
        d_model, _, inner = w_zx.shape
        heads = w_dt.shape[1]
        hd = inner // heads
        ns = STATE_DIM
        width = inner + 2 * ns
        sp = lax.axis_index('sp')
        x_blk = lax.all_gather(x_loc, 'tp', axis=0, tiled=True)
        n_tok = x_blk.shape[0]
        part = w_out.shape[0] // seq_blocks
        w_part = lax.dynamic_slice_in_dim(w_out, sp * part, part, axis=0)
        w_part, x_gate = lax.optimization_barrier((w_part, x_blk))
        w_all = lax.all_gather(w_part, ('tp', 'sp'), axis=0, tiled=True)
        seg_blk = lax.all_gather(seg_loc, 'tp', axis=0, tiled=True)
        to_next = [(s, s + 1) for s in range(seq_blocks - 1)]
        seg_tail = lax.ppermute(seg_blk[n_tok - 8:], 'sp', to_next)
        x_tail = lax.ppermute(x_gate[n_tok - 8:], 'sp', to_next)
        first = sp == 0
        seg_prev = jnp.where(first, seg_blk[0] - 1, seg_tail[7])
        segrel = seg_blk - seg_prev
        padded = jnp.concatenate([jnp.where(first, seg_blk[0] - 1, seg_tail[5:]), seg_blk])
        dist = sum((padded[3 - j:3 - j + n_tok] == seg_blk).astype(jnp.int32) for j in (1, 2, 3))
        comb = jnp.broadcast_to((segrel * 4 + dist)[:, None], (n_tok, CH))
        comb_row = segrel.reshape(n_tok // CH, 1, CH)
        w_bc2 = w_bc.reshape(d_model, 2 * ns)
        w_main = jnp.concatenate([w_zx[:, 1, :], w_bc2, jnp.tile(w_dt, (1, CH // heads))], axis=1)
        w_z = w_zx[:, 0, :]
        cw = jnp.concatenate([conv_x, conv_bc.reshape(CONV_WIDTH, 2 * ns)], axis=1).astype(F32)
        cb = jnp.concatenate([bias_x, bias_bc.reshape(2 * ns)])[None].astype(F32)
        cw = 0.5 * jnp.concatenate([cw, cb, jnp.zeros((3, width), F32)], axis=0)
        dtp, dskip, expm = head_tables(heads, inner, a_log, dt_bias, d_skip)
        halo = dotf(x_tail, w_main[:, :width]).astype(BF16)
        proj = dotf(x_gate, w_main).astype(BF16)
        y_loc, c_act, corr, end, dec = ssd_call(proj, comb, comb_row, halo, cw, dtp, dskip, expm, heads=heads, inner=inner, ns=ns)
        dec_row = jnp.repeat(dec[0:1, :heads], hd, axis=1)
        packed = jnp.concatenate([end, jnp.broadcast_to(dec_row, (8, inner))], axis=0)
        gathered = lax.all_gather(packed, 'sp', axis=0, tiled=False)
        x_z, _ = lax.optimization_barrier((x_gate, end))
        z = dotf(x_z, w_z).astype(BF16)
        st = jnp.zeros((ns, inner), F32)
        for src in range(seq_blocks - 1):
            nxt = gathered[src, ns:ns + 1] * st + gathered[src, :ns]
            st = jnp.where(src < sp, nxt, st)
        v = gate_call(y_loc, c_act, corr, z, st.astype(BF16), norm_w.astype(F32)[None], expm, heads=heads, eps=NORM_EPS)
        v_all = lax.all_to_all(v.reshape(head_shards, n_tok // head_shards, inner), 'tp', split_axis=0, concat_axis=0, tiled=False)
        out = jnp.einsum('stc,scd->td', v_all, w_all.reshape(head_shards, inner, d_model), preferred_element_type=F32)
        return (x_loc.astype(F32) + out).astype(BF16)

    return jax.shard_map(body, mesh=mesh, in_specs=(token_spec, seg_spec) + weight_specs, out_specs=token_spec, check_vma=False)
```

time: 2950 us -> 1030 us (0.35)
  local copies, waits for them, and re-layouts: 1150 us -> 53.2 us
  waiting for transfers between devices: 916 us -> 231 us
  blocking collectives: 19 us -> 297 us
  matrix products: 523 us -> 278 us
  other arithmetic: 229 us -> 4.28 us
  Pallas kernels: 0 us -> 139 us
  loops' own time: 42.3 us -> 0 us
    dynamic_update_slice x64 -> x0, local copies, waits for them, and re-layouts: 816 us -> none  [block_ssd(): end_state, y_tiles = lax.scan(body, init_state, tiles_in)]
    reduce_scatter x1 -> x0, waiting for transfers between devices: 643 us -> none  [body(): out_loc = lax.psum_scatter(out_part, 'tp', scatter_dimension=0, tiled=True)]
    all_to_all x0 -> x1, blocking collectives: none -> 278 us  [body(): lax.all_to_all(v.reshape(head_shards, n_tok // head_shards, inner), 'tp',...]
    dot_general x133 -> x4, matrix products: 523 us -> 278 us  [the longest x3 198 us: dotf(): return jnp.dot(a, b, preferred_element_type=F32)]
    pallas_call x0 -> x2, Pallas kernels: none -> 139 us  [the longest x1 99.6 us: ssd_call(): pl.pallas_call(kern, grid=(n_tok // rows,), in_specs=[pl.BlockSpec((rows,...]
    reshape x37 -> x0, local copies, waits for them, and re-layouts: 76.4 us -> none  [the longest x1 35.9 us: block_ssd(): return (end_state, y_tiles.reshape(row_count, groups, per_group, head_dim))]
    convert_element_type x7 -> x4, other arithmetic: 73.8 us -> 1.68 us  [the longest x1 1.52 us: body(): st.astype(BF16)]
    dynamic_slice x128 -> x1, local copies, waits for them, and re-layouts: 70.9 us -> 3.15 us  [body(): w_part = lax.dynamic_slice_in_dim(w_out, sp * part, part, axis=0)]
  transfers between devices with their start and end apart: 10 -> 5, of which waited for: 4 -> 1; matrix products, arithmetic and copies ran while one was open for 11% -> 24% of each run, Pallas kernels for 0% -> 4%
where the time goes in v1:
time: 1030 us; the launch traced here: 1020 us
  blocking collectives  297 us (29%)
  matrix products  278 us (27%)
  waiting for transfers between devices  231 us (22%)
  Pallas kernels  139 us (13%)
  local copies, waits for them, and re-layouts  53.2 us (5%)
  between operations  14.7 us (1%)
    all_to_all x1, blocking collectives, body(): lax.all_to_all(v.reshape(head_shards, n_tok // head_shards, inner), 'tp',...  278 us
    all_gather x1, waiting for transfers between devices, body(): x_blk = lax.all_gather(x_loc, 'tp', axis=0, tiled=True)  229 us
    dot_general x3, matrix products, dotf(): return jnp.dot(a, b, preferred_element_type=F32)  198 us
    pallas_call x1, Pallas kernels, ssd_call(): pl.pallas_call(kern, grid=(n_tok // rows,), in_specs=[pl.BlockSpec((rows,...  99.6 us
    dot_general x1, matrix products, body(): jnp.einsum('stc,scd->td', v_all, w_all.reshape(head_shards, inner, d_mode...  80 us
    pallas_call x1, Pallas kernels, gate_call(): pl.pallas_call(functools.partial(gate_kernel, heads=heads, eps=eps), grid...  38.9 us
    slice x1, local copies, waits for them, and re-layouts, body(): w_z = w_zx[:, 0, :]  32.5 us
  transfers between devices with their start and end apart: 5, of which 1 were waited for; matrix products, arithmetic and copies ran while one was open for 24% of the time, Pallas kernels for 4%

profile of v1, /device:TPU:97, one launch (start us, length us, event | category | flops | bytes accessed | tf_op | source)
XLA Modules:
  0.0 1024.8 jit_solution(9723986535234149524)
XLA Ops:
  6.5 0.0 all-gather.5.cloned.1.call-start
  6.6 0.7 all-gather.5.cloned.1.call-update
  7.3 0.1 all-gather.9.cloned.1.call-start
  7.4 19.0 %all_gather.16 = s32[8192]{0:T(1024)S(1)} all-gather(s32[1024]{0:T(1024)} %param.15), channel_id=1, replica_groups=mesh['dp'=1,'sp'=4,'tp'=8] {'tp'}, dimensions={0}, use_global_device_ids=true | all-gather | bytes 36864 | tf_op jit(solution)/shard_map/all_gather | solution.py:241
  26.4 0.1 slice.75
  26.4 3.8 collective-permute-start
  30.2 0.6 slice.74
  30.8 32.5 %fusion.30 = (bf16[4096,1,1024]{2,1,0:T(2,128)(2,1)}, bf16[4096,1,1024]{2,1,0:T(2,128)(2,1)S(1)}) fusion(bf16[4096,2,1024]{2,1,0:T(2,128)(2,1)} %param.16), kind=kLoop, calls=%fused_computation.63 | loop fusion | bytes 33554432 | tf_op jit(solution)/shard_map/slice | solution.py:254
  63.3 0.0 copy-start.2
  63.3 0.0 copy-start.5
  63.3 0.0 copy-start.9
  63.4 0.0 copy-start.7
  63.4 0.0 copy-start.12
  63.4 0.0 copy-start.13
  63.4 0.0 copy-start.10
  63.4 0.0 copy-start.11
  63.4 0.0 copy-start.6
  63.4 6.3 copy.33
  69.8 0.0 copy-done.2
  69.8 1.6 copy.34
  71.3 0.0 copy-done.5
  71.3 0.1 tile.8
  71.4 0.7 copy.20
  72.1 0.0 copy-done.9
  72.1 0.0 copy-done.7
  72.2 0.1 broadcast_in_dim_tile.7
  72.3 0.1 broadcast_in_dim_tile.6
  72.4 0.1 pad.7.clone
  72.4 0.1 pad.4.clone
  72.5 0.1 broadcast_in_dim.46
  72.6 0.1 broadcast_in_dim_reshape.3.dskip_ref
  73.3 0.1 maximum_maximum_fusion.dtp_ref
  73.5 0.1 and_convert_fusion.exp_ref
  73.6 0.1 maximum_multiply_fusion.cw_ref
  73.7 3.1 constant_dynamic-slice_fusion
  76.8 0.0 collective-permute-done
  76.8 0.6 slice.59
  78.1 0.1 broadcast_select_fusion
  78.2 0.7 broadcast_subtract_fusion
  78.9 229.2 %all-gather.5.cloned.1.call-done = bf16[8192,4096]{1,0:T(8,128)(2,1)} async-done(((bf16[1024,4096]{1,0:T(8,128)(2,1)}), bf16[8192,4096]{1,0:T(8,128)(2,1)}) %all-gather.5.cloned.1.call-update) | async-done | bytes 67108880 | tf_op jit(solution)/shard_map/all_gather | solution.py:235
  308.1 1.5 slice.64
  309.6 3.8 collective-permute-start.1
  313.3 113.1 %convolution_convert_fusion.xs_ref.bc_ref.dt_ref = bf16[8192,1408]{1,0:T(8,128)(2,1)} fusion(bf16[8192,4096]{1,0:T(8,128)(2,1)} %all-gather.5.cloned.1.call-done, bf16[4096,128]{1,0:T(8,128)(2,1)S(1)} %copy.20, bf16[4096,256]{1,0:T(8,128)(2,1)} %bitcast.73, bf16[4096,1024]{1,0:T(8,128)(2,1)} %bitcast.69), kind=kOutput, calls=%fused_computation | convolution fusion | flops 94535417856 | bytes 101711872 | tf_op jit(solution)/shard_map/dot_general | solution.py:18
  426.5 0.0 collective-permute-done.1
  426.5 4.9 fusion.10.halo_ref
  431.4 0.0 copy-done.4
  431.4 1.2 broadcast_in_dim.43.comb_ref
  432.6 0.0 copy-start.8
  432.6 99.6 %ssd.1 = (f32[8192,1024]{1,0:T(8,128)}, bf16[8192,128]{1,0:T(8,128)(2,1)S(1)}, f32[8192,128]{1,0:T(8,128)S(1)}, f32[128,1024]{1,0:T(8,128)S(1)}, f32[8,128]{1,0:T(8,128)S(1)}) custom-call(bf16[8192,1408]{1,0:T(8,128)(2,1)} %convolution_convert_fusion.xs_ref.bc_ref.dt_ref, bf16[8192,1408]{1,0:T(8,128)(2,1)} %convolution_convert_fusion.xs_ref.bc_ref.dt_ref, ...), custom_call_target="tpu_custom_call" | custom-call | flops 16384000000 | bytes 65536000 | tf_op jit(solution)/shard_map/ssd/pallas_call | solution.py:137
  532.2 2.0 copy-done
  534.3 0.1 broadcast_in_dim.47
  534.3 0.1 broadcast_in_dim.48
  534.4 0.8 pad_maximum_fusion
  535.3 0.1 all-gather.9.cloned.1.call-update
  535.3 0.1 all-gather.7.cloned.1.call-start
  535.4 0.7 all-gather.7.cloned.1.call-update
  536.1 80.4 %convolution_convert_fusion.1.z_ref = bf16[8192,1024]{1,0:T(8,128)(2,1)} fusion(bf16[8192,4096]{1,0:T(8,128)(2,1)} %all-gather.5.cloned.1.call-done, bf16[4096,1,1024]{2,1,0:T(2,128)(2,1)} %get-tuple-element.21), kind=kOutput, calls=%fused_computation.3 | convolution fusion | flops 68727865344 | bytes 92274688 | tf_op jit(solution)/shard_map/dot_general | solution.py:18
  616.5 0.8 fusion.31
  617.3 1.5 fusion.15.st_ref
  618.8 0.0 copy-start.1
  618.8 2.2 copy-done.1
  621.0 38.9 %gate.1 = bf16[8192,1024]{1,0:T(8,128)(2,1)} custom-call(f32[8192,1024]{1,0:T(8,128)} %get-tuple-element.14.y_ref, bf16[8192,128]{1,0:T(8,128)(2,1)S(1)} %get-tuple-element.15.c_ref, f32[8192,128]{1,0:T(8,128)S(1)} %copy-done.1, bf16[8192,1024]{1,0:T(8,128)(2,1)} %convolution_convert_fusion.1.z_ref, bf16[128,1024]{1,0:T(8,128)(2,1)S(1)} %fusion.15.st_ref, ...), custom_call_target="tpu_custom_call" | custom-call | flops 4096000000 | bytes 65536000 | tf_op jit(solution)/shard_map/gate/pallas_call | solution.py:191
  660.0 278.3 %all_to_all.5 = bf16[8,1024,1024]{2,1,0:T(8,128)(2,1)} all-to-all(bf16[8,1024,1024]{2,1,0:T(8,128)(2,1)} %bitcast.68), channel_id=1, replica_groups=mesh['dp'=1,'sp'=4,'tp'=8] {'tp'}, dimensions={0} | all-to-all | bytes 33554432 | tf_op jit(solution)/shard_map/all_to_all | solution.py:272
  938.3 80.0 %fusion = bf16[1024,4096]{1,0:T(8,128)(2,1)} fusion(bf16[1024,4096]{1,0:T(8,128)(2,1)} %param.14, bf16[8,1024,1024]{2,1,0:T(8,128)(2,1)} %all_to_all.5, bf16[8,1024,4096]{2,1,0:T(8,128)(2,1)} %bitcast.16), kind=kOutput, calls=%fused_computation.2 | convolution fusion | flops 68732059648 | bytes 100663296 | tf_op jit(solution)/shard_map/stc,scd->td/dot_general | solution.py:273
  (28 shorter events, 0.1 us)
Async XLA Ops:
  6.5 301.5 %all-gather.5.cloned.1.call-start = ((), (), s32[]{:S(2)}) async-start(), calls=%async_computation.1 | async-start | bytes 75497472 | tf_op jit(solution)/shard_map/all_gather | solution.py:235
  7.3 609.2 %all-gather.9.cloned.1.call-start = ((), (), s32[]{:S(2)}) async-start(), calls=%async_computation.3 | async-start | bytes 2785280 | tf_op jit(solution)/shard_map/all_gather | solution.py:264
  26.4 50.4 %collective-permute-start = (s32[8]{0:T(128)S(1)}, s32[8]{0:T(128)S(1)}, u32[]{:S(2)}, u32[]{:S(2)}) collective-permute-start(s32[8]{0:T(128)S(1)} %slice.75), channel_id=1, source_target_pairs={{0,8},{8,16},{16,24},{1,9},{9,17},{17,25},{2,10},{10,18},{18,26},{... | collective-permute-start | bytes 104 | tf_op jit(solution)/shard_map/ppermute | solution.py:243
  63.3 6.4 copy-start.2
  63.3 8.0 copy-start.5
  63.3 8.8 copy-start.9
  63.4 8.8 copy-start.7
  63.4 8.8 copy-start.12
  63.4 8.8 copy-start.13
  63.4 8.9 copy-start.10
  63.4 9.1 copy-start.11
  63.4 10.0 copy-start.6
  309.6 116.9 %collective-permute-start.1 = (bf16[8,4096]{1,0:T(8,128)(2,1)}, bf16[8,4096]{1,0:T(8,128)(2,1)}, u32[]{:S(2)}, u32[]{:S(2)}) collective-permute-start(bf16[8,4096]{1,0:T(8,128)(2,1)} %slice.64), channel_id=1, source_target_pairs={{0,8},{8,16},{16,24},{1,9},{9,17},{17,25},{2,10},{10,18},{18,26},{... | collective-permute-start | bytes 196616 | tf_op jit(solution)/shard_map/ppermute | solution.py:244
  313.3 113.2 %copy-start.3 = (bf16[512,8,2,128]{3,1,2,0:T(8,128)(2,1)S(1)}, bf16[512,8,2,128]{3,1,2,0:T(8,128)(2,1)}, u32[]{:S(2)}) copy-start(bf16[512,8,2,128]{3,1,2,0:T(8,128)(2,1)} %copy.34) | copy-start | bytes 6291460
  313.3 118.0 %copy-start.4 = (s32[8192]{0:T(1024)S(1)}, s32[8192]{0:T(1024)}, u32[]{:S(2)}) copy-start(s32[8192]{0:T(1024)} %get-tuple-element.27) | copy-start | bytes 98308
  432.6 103.5 %copy-start.8 = (bf16[1024]{0:T(1024)(128)(2,1)S(1)}, bf16[1024]{0:T(1024)(128)(2,1)}, u32[]{:S(2)}) copy-start(bf16[1024]{0:T(1024)(128)(2,1)} %param.26) | copy-start | bytes 6148
  532.2 2.0 copy-start
  535.3 402.9 %all-gather.7.cloned.1.call-start = ((), (), s32[]{:S(2)}) async-start(), calls=%async_computation.2 | async-start | bytes 69206016 | tf_op jit(solution)/shard_map/all_gather | solution.py:240
  618.8 2.2 copy-start.1
Sparse Core Ops, SparseCore 0:
  9.0 299.0 all-gather.4
  535.4 28.3 all-gather.8
  565.9 367.6 all-gather.6
